TPU v7x, 32 devices: a whole 2x2x4 slice. The times are simulated.
32 devices in a mesh: dp: 4 (over y, core), tp: 8 (over z, x).
Axes of the slice: x: 2, y: 2, z: 4, core: 2. Of those that a mesh axis runs over, the one named last changes fastest.
Arguments:
- inputs: bfloat16 [4, 8, 8192], P('dp', 'tp'), may hold values from -134 to 134, as said below
- norm_gain: float32 [8192], replicated, may hold values from 0.1 to 1.9
- gate_grad: bfloat16 [4, 8, 16384], P('dp', None, 'tp'), may hold values from -36 to 36
- up_grad: bfloat16 [4, 8, 16384], P('dp', None, 'tp'), may hold values from -36 to 36
- gate_weight: bfloat16 [8192, 16384], P(None, 'tp'), may hold values from -0.046875 to 0.046875
- up_weight: bfloat16 [8192, 16384], P(None, 'tp'), may hold values from -0.046875 to 0.046875
Outputs:
- input_grad: bfloat16 [4, 8, 8192], P('dp', 'tp')
- gain_grad: float32 [8192], replicated
Inputs may be any that keep to these rules, and one draw needn't show every extreme that they name: `inputs`: activations with token and feature scales.
All inputs are finite; a program needn't handle non-finite values.
Results may differ from a plain program's by a relative error of at most 0.00165.
Values may be sent and summed in bfloat16 or wider, within the bound.
A program may use at most 128 MiB of HBM per device.

v0:
```python
import functools

import jax
import jax.numpy as jnp
from jax import lax
from jax.experimental import pallas as pl
from jax.experimental.pallas import tpu as pltpu
from jax.sharding import PartitionSpec as P

epsilon = 1e-05
MESH = pl.DeviceIdType.MESH
NT = (((1,), (1,)), ((), ()))


def normalize(values):
    inv_rms = lax.rsqrt(jnp.mean(values * values, axis=-1, keepdims=True) + epsilon)
    return (inv_rms, values * inv_rms)


def plain(inputs, norm_gain, gate_grad, up_grad, gate_weight, up_weight):
    seq = gate_grad.shape[1]
    width = gate_weight.shape[0]
    cot_gate = gate_grad.reshape(-1, gate_grad.shape[-1])
    cot_up = up_grad.reshape(-1, up_grad.shape[-1])
    inv_rms, normed = normalize(inputs.astype(jnp.float32))
    full_term = lax.dot_general(cot_gate, gate_weight, NT, preferred_element_type=jnp.float32)
    full_term = full_term + lax.dot_general(cot_up, up_weight, NT, preferred_element_type=jnp.float32)
    full_term = full_term.reshape(-1, seq, width)
    row_grad = lax.psum_scatter(full_term, "tp", scatter_dimension=1, tiled=True)
    gain_grad = lax.psum(jnp.sum(row_grad * normed, axis=(0, 1)), ("dp", "tp"))
    scaled = row_grad * norm_gain
    inner = jnp.mean(scaled * normed, axis=-1, keepdims=True)
    return ((inv_rms * (scaled - normed * inner)).astype(jnp.bfloat16), gain_grad)


def kernel(
    n_dp, n_tp, x_ref, gain_ref, gg_ref, ug_ref, gw_ref, uw_ref, dx_ref, dg_ref,
    w_buf, cot, g_mat, x_row, x_send, x_recv, x_mat, part_send, part_recv, last_send, last_recv,
    w_sem, own_sem, row_sem, cot_ss, cot_rs, x_ss, x_rs, part_ss, part_rs, last_ss, last_rs,
):
    n = n_dp * n_tp
    d, t = lax.axis_index("dp"), lax.axis_index("tp")
    me = d * n_tp + t
    seq = gg_ref.shape[1]
    width = gw_ref.shape[0]
    cut = width // n
    base = d * (n_tp * cut)

    def place(flat):
        return {"dp": lax.div(flat, n_tp), "tp": lax.rem(flat, n_tp)}

    barrier = pltpu.get_barrier_semaphore()

    @pl.loop(1, n)
    def _(k):
        pl.semaphore_signal(barrier, inc=1, device_id=place(lax.rem(me + k, n)), device_id_type=MESH)

    own = [
        pltpu.make_async_copy(gg_ref.at[0], cot.at[d, 0], own_sem.at[0]),
        pltpu.make_async_copy(ug_ref.at[0], cot.at[d, 1], own_sem.at[1]),
        pltpu.make_async_copy(x_ref, x_row, row_sem),
    ]
    for copy in own:
        copy.start()

    def peer(k):
        to = t
        for bit in range(n_tp.bit_length() - 1):
            if k >> bit & 1:
                to = to + 2**bit - 2 ** (bit + 1) * lax.rem(lax.div(to, 2**bit), 2)
        return to

    order = sorted(range(n_tp), key=lambda k: -(k.bit_length()))

    def weight_copy(i, which):
        rows = pl.ds(pl.multiple_of(base + peer(order[i]) * cut, cut), cut)
        source = (gw_ref, uw_ref)[which]
        return pltpu.make_async_copy(source.at[rows, :], w_buf.at[i, which], w_sem.at[i, which])

    for copy in own:
        copy.wait()
    for which in range(2):
        for i in range(n_tp):
            weight_copy(i, which).start()

    pl.semaphore_wait(barrier, n - 1)

    def cot_copy(step, which):
        to = lax.rem(d + step, n_dp)
        return pltpu.make_async_remote_copy(
            src_ref=cot.at[d, which], dst_ref=cot.at[d, which],
            send_sem=cot_ss.at[which, to], recv_sem=cot_rs.at[which, d],
            device_id={"dp": to, "tp": t}, device_id_type=MESH,
        )

    def cot_arrival(step, which):
        source = lax.rem(d + step, n_dp)
        return pltpu.make_async_remote_copy(
            src_ref=cot.at[source, which], dst_ref=cot.at[source, which],
            send_sem=cot_ss.at[which, source], recv_sem=cot_rs.at[which, source],
            device_id={"dp": source, "tp": t}, device_id_type=MESH,
        )

    for which in range(2):
        for step in range(1, n_dp):
            cot_copy(step, which).start()

    squares = jnp.zeros((1, cut), jnp.float32)
    for i in range(n):
        piece = x_row[0, :, i * cut:(i + 1) * cut].astype(jnp.float32)
        x_send[i] = piece
        squares = squares + piece * piece
    inv_rms = lax.rsqrt(jnp.sum(squares, axis=1, keepdims=True) / width + epsilon)
    for i in range(n):
        x_send[i] = x_send[i] * inv_rms

    def spread(send, recv, send_sem, recv_sem, k):
        to = lax.rem(me + k, n)
        return pltpu.make_async_remote_copy(
            src_ref=send.at[to], dst_ref=recv.at[me], send_sem=send_sem.at[to], recv_sem=recv_sem.at[me],
            device_id=place(to), device_id_type=MESH,
        )

    def arrival(send, recv, send_sem, recv_sem, k):
        source = lax.rem(me + k, n)
        return pltpu.make_async_remote_copy(
            src_ref=send.at[source], dst_ref=recv.at[source], send_sem=send_sem.at[source],
            recv_sem=recv_sem.at[source], device_id=place(source), device_id_type=MESH,
        )

    @pl.loop(1, n)
    def _(k):
        spread(x_send, x_recv, x_ss, x_rs, k).start()

    x_recv[me] = x_send[me]

    def gather(which):
        for step in range(1, n_dp):
            cot_arrival(step, which).wait_recv()
        for row in range(n_dp):
            g_mat[which, row * seq:(row + 1) * seq, :] = cot[row, which]

    def product(i, which):
        return lax.dot_general(g_mat[which], w_buf[i, which], NT, preferred_element_type=jnp.float32)

    half, pair = n_tp // 2, 2
    gather(0)
    for i in range(n_tp):
        weight_copy(i, 0).wait()
    for i in range(half):
        part_send[i] = product(i, 0)

    def part_copy(i):
        return pltpu.make_async_remote_copy(
            src_ref=part_send.at[i], dst_ref=part_recv.at[i], send_sem=part_ss.at[i], recv_sem=part_rs.at[i],
            device_id={"dp": d, "tp": peer(order[i])}, device_id_type=MESH,
        )

    gather(1)
    for i in range(n_tp):
        weight_copy(i, 1).wait()
    for low in range(0, n_tp, pair):
        for i in range(low, low + pair):
            if i < half:
                part_send[i] = part_send[i] + product(i, 1)
            else:
                part_send[i] = product(i, 0) + product(i, 1)
        for i in range(low, low + pair):
            if i < n_tp - 1:
                part_copy(i).start()
    total = part_send[n_tp - 1]

    @pl.loop(1, n)
    def _(k):
        arrival(x_send, x_recv, x_ss, x_rs, k).wait_recv()

    for i in range(n):
        x_mat[i:i + 1, :] = x_recv[i]

    for i in range(n_tp - 1):
        part_copy(i).wait_recv()
        total = total + part_recv[i]

    gain_part = jnp.sum(total * x_mat[...], axis=0, keepdims=True)
    for i in range(n):
        last_send[i, 0] = total[i:i + 1, :]
        last_send[i, 1] = gain_part

    @pl.loop(1, n)
    def _(k):
        spread(last_send, last_recv, last_ss, last_rs, k).start()

    last_recv[me] = last_send[me]

    for which in range(2):
        for step in range(1, n_dp):
            cot_copy(step, which).wait_send()
    for i in range(n_tp - 1):
        part_copy(i).wait_send()

    @pl.loop(1, n)
    def _(k):
        spread(x_send, x_recv, x_ss, x_rs, k).wait_send()

    @pl.loop(1, n)
    def _(k):
        arrival(last_send, last_recv, last_ss, last_rs, k).wait_recv()

    dots = jnp.zeros((1, cut), jnp.float32)
    for i in range(n):
        dots = dots + last_recv[i, 0] * gain_ref[i] * x_send[i]
        dg_ref[i] = last_recv[i, 1]
    inner = jnp.sum(dots, axis=1, keepdims=True) / width
    for i in range(n):
        scaled = last_recv[i, 0] * gain_ref[i]
        dx_ref[0, :, i * cut:(i + 1) * cut] = (inv_rms * (scaled - x_send[i] * inner)).astype(jnp.bfloat16)

    @pl.loop(1, n)
    def _(k):
        spread(last_send, last_recv, last_ss, last_rs, k).wait_send()


def write_out(dx_ref, dg_ref, dx_out, dg_out):
    dx_out[...] = dx_ref[...]
    dg_out[...] = dg_ref[...]


def fused(n_dp, n_tp, inputs, norm_gain, gate_grad, up_grad, gate_weight, up_weight):
    n = n_dp * n_tp
    seq, depth = gate_grad.shape[1:]
    width = gate_weight.shape[0]
    cut = width // n
    rows = n_dp * seq
    dma, vmem = pltpu.SemaphoreType.DMA, pltpu.VMEM
    input_grad, gain_grad = pl.pallas_call(
        functools.partial(kernel, n_dp, n_tp),
        out_shape=(vmem(inputs.shape, jnp.bfloat16), vmem((n, 1, cut), jnp.float32)),
        in_specs=[pl.BlockSpec(memory_space=pl.ANY), pl.BlockSpec(memory_space=vmem)]
        + [pl.BlockSpec(memory_space=pl.ANY)] * 4,
        out_specs=(pl.BlockSpec(memory_space=vmem),) * 2,
        scratch_shapes=[
            vmem((n_tp, 2, cut, depth), jnp.bfloat16),
            vmem((n_dp, 2, seq, depth), jnp.bfloat16),
            vmem((2, rows, depth), jnp.bfloat16),
            vmem(inputs.shape, jnp.bfloat16),
            vmem((n, 1, cut), jnp.float32),
            vmem((n, 1, cut), jnp.float32),
            vmem((n, cut), jnp.float32),
            vmem((n_tp, rows, cut), jnp.float32),
            vmem((n_tp, rows, cut), jnp.float32),
            vmem((n, 2, 1, cut), jnp.float32),
            vmem((n, 2, 1, cut), jnp.float32),
            dma((n_tp, 2)), dma((2,)), dma,
            dma((2, n_dp)), dma((2, n_dp)),
            dma((n,)), dma((n,)),
            dma((n_tp,)), dma((n_tp,)),
            dma((n,)), dma((n,)),
        ],
        compiler_params=pltpu.CompilerParams(collective_id=0, has_side_effects=True),
    )(inputs, norm_gain.reshape(n, 1, cut), gate_grad, up_grad, gate_weight, up_weight)
    input_grad, gain_grad = pl.pallas_call(
        write_out,
        out_shape=(
            jax.ShapeDtypeStruct(inputs.shape, jnp.bfloat16),
            jax.ShapeDtypeStruct((n, 1, cut), jnp.float32),
        ),
        in_specs=[pl.BlockSpec(memory_space=vmem)] * 2,
        out_specs=(pl.BlockSpec(memory_space=vmem),) * 2,
        compiler_params=pltpu.CompilerParams(vmem_limit_bytes=2**20),
    )(input_grad, gain_grad)
    return (input_grad, gain_grad.reshape(width))


def per_device(n_dp, n_tp, *args):
    inputs, gate_grad, gate_weight = args[0], args[2], args[4]
    n = n_dp * n_tp
    width, depth = gate_weight.shape
    fits = (
        inputs.shape[:2] == (1, 1)
        and gate_grad.shape[0] == 1
        and gate_grad.shape[1] == n_tp
        and n_tp % 8 == 0
        and n_tp & (n_tp - 1) == 0
        and width % (n * 128) == 0
        and depth % 256 == 0
        and width // n_dp * depth * 4 <= 40 * 2**20
    )
    return fused(n_dp, n_tp, *args) if fits else plain(*args)


def solution(mesh):
    return jax.shard_map(
        functools.partial(per_device, mesh.shape["dp"], mesh.shape["tp"]),
        mesh=mesh,
        in_specs=(
            P("dp", "tp", None),
            P(),
            P("dp", None, "tp"),
            P("dp", None, "tp"),
            P(None, "tp"),
            P(None, "tp"),
        ),
        out_specs=(P("dp", "tp", None), P()),
        check_vma=False,
    )
```

profile of v0, /device:TPU:0, one launch (start us, length us, event | category | flops | bytes accessed | tf_op | source)
XLA Modules:
  0.0 29.0 jit_solution(1237554297534441395)
XLA Ops:
  0.6 27.7 %shard_map.77 = (bf16[1,1,8192]{2,1,0:T(2,128)(2,1)S(1)}, f32[32,1,256]{2,1,0:T(1,128)S(1)}) custom-call(bf16[1,1,8192]{2,1,0:T(2,128)(2,1)} %x_ref.1, f32[32,1,256]{2,1,0:T(1,128)} %bitcast.2, bf16[1,8,2048]{2,1,0:T(8,128)(2,1)} %gg_ref.1, bf16[1,8,2048]{2,1,0:T(8,128)(2,1)} %ug_ref.1, bf16[8192,2048]{1,0:T(8,128)(2,1)} %gw_ref.1, bf16[8192,2048]{1,0:T(8,128)(2,1)} %uw_ref.1), custom_call_target="tpu_custom_call" | custom-call | tf_op jit(solution)/shard_map/pallas_call | solution.py:235
  28.4 0.6 %shard_map.78 = (bf16[1,1,8192]{2,1,0:T(2,128)(2,1)}, f32[32,1,256]{2,1,0:T(1,128)}) custom-call(bf16[1,1,8192]{2,1,0:T(2,128)(2,1)S(1)} %get-tuple-element.6.dx_ref, f32[32,1,256]{2,1,0:T(1,128)S(1)} %get-tuple-element.7.dg_ref), custom_call_target="tpu_custom_call" | custom-call | tf_op jit(solution)/shard_map/pallas_call | solution.py:261
where the time goes:
time: 29.3 us; the launch traced here: 29 us
  Pallas kernels  28.4 us (97%)
  between operations  0.64 us (2%)
    pallas_call x1, Pallas kernels, fused(): pl.pallas_call(functools.partial(kernel, n_dp, n_tp), out_shape=(vmem(inp...  27.7 us
    pallas_call x1, Pallas kernels, fused(): pl.pallas_call(write_out, out_shape=(jax.ShapeDtypeStruct(inputs.shape, j...  0.64 us

commit v1 on v0

v1 whole, which is shorter than its diff:
```python
import functools

import jax
import jax.numpy as jnp
from jax import lax
from jax.experimental import pallas as pl
from jax.experimental.pallas import tpu as pltpu
from jax.sharding import PartitionSpec as P

epsilon = 1e-05
MESH = pl.DeviceIdType.MESH
NT = (((1,), (1,)), ((), ()))


def normalize(values):
    inv_rms = lax.rsqrt(jnp.mean(values * values, axis=-1, keepdims=True) + epsilon)
    return (inv_rms, values * inv_rms)


def plain(inputs, norm_gain, gate_grad, up_grad, gate_weight, up_weight):
    seq = gate_grad.shape[1]
    width = gate_weight.shape[0]
    cot_gate = gate_grad.reshape(-1, gate_grad.shape[-1])
    cot_up = up_grad.reshape(-1, up_grad.shape[-1])
    inv_rms, normed = normalize(inputs.astype(jnp.float32))
    full_term = lax.dot_general(cot_gate, gate_weight, NT, preferred_element_type=jnp.float32)
    full_term = full_term + lax.dot_general(cot_up, up_weight, NT, preferred_element_type=jnp.float32)
    full_term = full_term.reshape(-1, seq, width)
    row_grad = lax.psum_scatter(full_term, "tp", scatter_dimension=1, tiled=True)
    gain_grad = lax.psum(jnp.sum(row_grad * normed, axis=(0, 1)), ("dp", "tp"))
    scaled = row_grad * norm_gain
    inner = jnp.mean(scaled * normed, axis=-1, keepdims=True)
    return ((inv_rms * (scaled - normed * inner)).astype(jnp.bfloat16), gain_grad)


def kernel(
    n_dp, n_tp, x_ref, gain_hbm, gg_ref, ug_ref, gw_ref, uw_ref, dx_ref, dg_ref,
    w_buf, cot, g_mat, x_row, gain_ref, x_send, x_recv, x_mat, acc, part_send, part_recv, last_send, last_recv,
    w_sem, own_sem, row_sem, known, cot_ss, cot_rs, x_ss, x_rs, part_ss, part_rs, last_ss, last_rs,
):
    n = n_dp * n_tp
    bits = n_tp.bit_length() - 1
    d, t = lax.axis_index("dp"), lax.axis_index("tp")
    me = d * n_tp + t
    seq = gg_ref.shape[1]
    width = gw_ref.shape[0]
    cut = width // n
    base = d * (n_tp * cut)

    def flip(to, k):
        for bit in range(bits):
            if k >> bit & 1:
                to = to + 2**bit - 2 ** (bit + 1) * lax.rem(lax.div(to, 2**bit), 2)
        return to

    partners = [flip(t, k) for k in range(n_tp)]
    rows_of = [lax.rem(d + step, n_dp) for step in range(n_dp)]

    own = [
        pltpu.make_async_copy(gg_ref.at[0], cot.at[d, 0], own_sem.at[0]),
        pltpu.make_async_copy(ug_ref.at[0], cot.at[d, 1], own_sem.at[1]),
        pltpu.make_async_copy(x_ref, x_row, row_sem.at[0]),
        pltpu.make_async_copy(gain_hbm, gain_ref, row_sem.at[1]),
    ]
    with jax.named_scope("own_start"):
        for copy in own:
            copy.start()

    with jax.named_scope("greet"):
        barrier = pltpu.get_barrier_semaphore()
        for bit in range(bits):
            pl.semaphore_signal(barrier, inc=1, device_id={"dp": d, "tp": partners[2**bit]}, device_id_type=MESH)
        for step in range(1, n_dp):
            pl.semaphore_signal(barrier, inc=1, device_id={"dp": rows_of[step], "tp": t}, device_id_type=MESH)


    order = sorted(range(n_tp), key=lambda k: -(k.bit_length()))
    half = n_tp // 2

    def weight_copy(i, which):
        rows = pl.ds(pl.multiple_of(base + partners[order[i]] * cut, cut), cut)
        source = (gw_ref, uw_ref)[which]
        return pltpu.make_async_copy(source.at[rows, :], w_buf.at[i, which], w_sem.at[i, which])

    stream = [(i, 0) for i in range(half)] + [(i, 1) for i in range(half)]
    stream += [(i, which) for i in range(half, n_tp) for which in range(2)]
    with jax.named_scope("w_start"):
        for i, which in stream:
            weight_copy(i, which).start()

    def cot_copy(step, which):
        to = rows_of[step]
        return pltpu.make_async_remote_copy(
            src_ref=cot.at[d, which], dst_ref=cot.at[d, which],
            send_sem=cot_ss.at[which, to], recv_sem=cot_rs.at[which, d],
            device_id={"dp": to, "tp": t}, device_id_type=MESH,
        )

    def cot_arrival(step, which):
        source = rows_of[step]
        return pltpu.make_async_remote_copy(
            src_ref=cot.at[source, which], dst_ref=cot.at[source, which],
            send_sem=cot_ss.at[which, source], recv_sem=cot_rs.at[which, source],
            device_id={"dp": source, "tp": t}, device_id_type=MESH,
        )

    with jax.named_scope("own_wait"):
        own[0].wait()
        own[1].wait()
    with jax.named_scope("bar_wait"):
        pl.semaphore_wait(barrier, bits + n_dp - 1)
    with jax.named_scope("cot_start"):
        for which in range(2):
            for step in range(1, n_dp):
                cot_copy(step, which).start()

    def tell(bit):
        pl.semaphore_signal(known.at[bit], inc=1, device_id={"dp": d, "tp": partners[2**bit]}, device_id_type=MESH)

    def part_copy(i):
        return pltpu.make_async_remote_copy(
            src_ref=part_send.at[i], dst_ref=part_recv.at[i], send_sem=part_ss.at[i], recv_sem=part_rs.at[i],
            device_id={"dp": d, "tp": partners[order[i]]}, device_id_type=MESH,
        )

    place = t * n_dp + d

    def other(k):
        flat = k + lax.div(k + n - place, n)
        to_t = lax.div(flat, n_dp)
        return flat - to_t * n_dp, to_t

    def spread(send, recv, send_sem, recv_sem, k):
        to_d, to_t = other(k)
        return pltpu.make_async_remote_copy(
            src_ref=send.at[to_d * n_tp + to_t], dst_ref=recv.at[me], send_sem=send_sem, recv_sem=recv_sem,
            device_id={"dp": to_d, "tp": to_t}, device_id_type=MESH,
        )

    def all_of(send, recv, send_sem, recv_sem):
        return pltpu.make_async_remote_copy(
            src_ref=send.at[pl.ds(0, n - 1)], dst_ref=recv.at[pl.ds(0, n - 1)], send_sem=send_sem,
            recv_sem=recv_sem, device_id={"dp": rows_of[1], "tp": t}, device_id_type=MESH,
        )

    def gather(which):
        for step in range(1, n_dp):
            cot_arrival(step, which).wait_recv()
        for row in range(n_dp):
            g_mat[which, row * seq:(row + 1) * seq, :] = cot[row, which]

    lanes = [slice(low, low + cut // 2) for low in range(0, cut, cut // 2)]

    def product(i, which, rows):
        return lax.dot_general(w_buf[i, which, rows, :], g_mat[which], NT, preferred_element_type=jnp.float32)

    tell(1)
    with jax.named_scope("x_norm"):
        own[2].wait()
        squares = jnp.zeros((1, cut), jnp.float32)
        for i in range(n):
            piece = x_row[0, :, i * cut:(i + 1) * cut].astype(jnp.float32)
            x_send[i] = piece
            squares = squares + piece * piece
        inv_rms = lax.rsqrt(jnp.sum(squares, axis=1, keepdims=True) / width + epsilon)
        for i in range(n):
            x_send[i] = x_send[i] * inv_rms
        x_recv[me] = x_send[me]
    with jax.named_scope("rounds"):
        for bit in range(1, bits):
            pl.semaphore_wait(known.at[bit], 1)
            if bit + 1 < bits:
                tell(bit + 1)
        for step in range(1, n_dp):
            pl.semaphore_signal(known.at[0], inc=1, device_id={"dp": rows_of[step], "tp": t}, device_id_type=MESH)
    with jax.named_scope("gather0"):
        gather(0)
        for i in range(half):
            weight_copy(i, 0).wait()
    with jax.named_scope("gate_far"):
        for i in range(half):
            for rows in lanes:
                acc[i, rows, :] = product(i, 0, rows)
    with jax.named_scope("known"):
        pl.semaphore_wait(known.at[0], n_dp - 1)
    with jax.named_scope("x_start"):
        for k in range(n - 1):
            spread(x_send, x_recv, x_ss, x_rs, k).start()
    with jax.named_scope("gather1"):
        gather(1)
        for i in range(half):
            weight_copy(i, 1).wait()
    with jax.named_scope("up_far"):
        for i in range(half):
            for rows in lanes:
                part_send[i, :, rows] = (acc[i, rows, :] + product(i, 1, rows)).T
            part_copy(i).start()
    with jax.named_scope("w_wait"):
        for i in range(half, n_tp):
            for which in range(2):
                weight_copy(i, which).wait()
    with jax.named_scope("near"):
        for i in range(half, n_tp):
            for rows in lanes:
                part_send[i, :, rows] = (product(i, 0, rows) + product(i, 1, rows)).T
            if i < n_tp - 1:
                part_copy(i).start()
    total = part_send[n_tp - 1]

    with jax.named_scope("x_wait"):
        all_of(x_send, x_recv, x_ss, x_rs).wait_recv()
    with jax.named_scope("x_mat"):
        for i in range(n):
            x_mat[i:i + 1, :] = x_recv[i]

    for i in reversed(range(n_tp - 1)):
        with jax.named_scope(f"part{i}"):
            part_copy(i).wait_recv()
            total = total + part_recv[i]

    with jax.named_scope("gain_part"):
        gain_part = jnp.sum(total * x_mat[...], axis=0, keepdims=True)
        for i in range(n):
            last_send[i, 0] = total[i:i + 1, :]
            last_send[i, 1] = gain_part
    with jax.named_scope("last_start"):
        for k in range(n - 1):
            spread(last_send, last_recv, last_ss, last_rs, k).start()

        last_recv[me] = last_send[me]

    with jax.named_scope("send_waits"):
        own[3].wait()
        for which in range(2):
            for step in range(1, n_dp):
                cot_copy(step, which).wait_send()
        for i in range(n_tp - 1):
            part_copy(i).wait_send()
        all_of(x_send, x_recv, x_ss, x_rs).wait_send()
        all_of(last_send, last_recv, last_ss, last_rs).wait_send()

    with jax.named_scope("last_wait"):
        all_of(last_send, last_recv, last_ss, last_rs).wait_recv()

    with jax.named_scope("finish"):
        dots = jnp.zeros((1, cut), jnp.float32)
        for i in range(n):
            dots = dots + last_recv[i, 0] * gain_ref[i] * x_send[i]
            dg_ref[i] = last_recv[i, 1]
        inner = jnp.sum(dots, axis=1, keepdims=True) / width
        for i in range(n):
            scaled = last_recv[i, 0] * gain_ref[i]
            dx_ref[0, :, i * cut:(i + 1) * cut] = (inv_rms * (scaled - x_send[i] * inner)).astype(jnp.bfloat16)


def write_out(dx_ref, dg_ref, dx_out, dg_out):
    dx_out[...] = dx_ref[...]
    dg_out[...] = dg_ref[...]


def fused(n_dp, n_tp, inputs, norm_gain, gate_grad, up_grad, gate_weight, up_weight):
    n = n_dp * n_tp
    seq, depth = gate_grad.shape[1:]
    width = gate_weight.shape[0]
    cut = width // n
    rows = n_dp * seq
    dma, vmem = pltpu.SemaphoreType.DMA, pltpu.VMEM
    input_grad, gain_grad = pl.pallas_call(
        functools.partial(kernel, n_dp, n_tp),
        out_shape=(vmem(inputs.shape, jnp.bfloat16), vmem((n, 1, cut), jnp.float32)),
        in_specs=[pl.BlockSpec(memory_space=pl.ANY)] * 6,
        out_specs=(pl.BlockSpec(memory_space=vmem),) * 2,
        scratch_shapes=[
            vmem((n_tp, 2, cut, depth), jnp.bfloat16),
            vmem((n_dp, 2, seq, depth), jnp.bfloat16),
            vmem((2, rows, depth), jnp.bfloat16),
            vmem(inputs.shape, jnp.bfloat16),
            vmem((n, 1, cut), jnp.float32),
            vmem((n, 1, cut), jnp.float32),
            vmem((n, 1, cut), jnp.float32),
            vmem((n, cut), jnp.float32),
            vmem((n_tp // 2, cut, rows), jnp.float32),
            vmem((n_tp, rows, cut), jnp.float32),
            vmem((n_tp, rows, cut), jnp.float32),
            vmem((n, 2, 1, cut), jnp.float32),
            vmem((n, 2, 1, cut), jnp.float32),
            dma((n_tp, 2)), dma((2,)), dma((2,)),
            pltpu.SemaphoreType.REGULAR((n_tp.bit_length(),)),
            dma((2, n_dp)), dma((2, n_dp)),
            dma, dma,
            dma((n_tp,)), dma((n_tp,)),
            dma, dma,
        ],
        compiler_params=pltpu.CompilerParams(collective_id=0, has_side_effects=True),
    )(inputs, norm_gain.reshape(n, 1, cut), gate_grad, up_grad, gate_weight, up_weight)
    input_grad, gain_grad = pl.pallas_call(
        write_out,
        out_shape=(
            jax.ShapeDtypeStruct(inputs.shape, jnp.bfloat16),
            jax.ShapeDtypeStruct((n, 1, cut), jnp.float32),
        ),
        in_specs=[pl.BlockSpec(memory_space=vmem)] * 2,
        out_specs=(pl.BlockSpec(memory_space=vmem),) * 2,
        compiler_params=pltpu.CompilerParams(vmem_limit_bytes=2**20),
    )(input_grad, gain_grad)
    return (input_grad, gain_grad.reshape(width))


def per_device(n_dp, n_tp, *args):
    inputs, gate_grad, gate_weight = args[0], args[2], args[4]
    n = n_dp * n_tp
    width, depth = gate_weight.shape
    fits = (
        inputs.shape[:2] == (1, 1)
        and gate_grad.shape[0] == 1
        and gate_grad.shape[1] == n_tp
        and n_tp % 8 == 0
        and n_tp & (n_tp - 1) == 0
        and width % (n * 128) == 0
        and depth % 256 == 0
        and width // n_dp * depth * 4 <= 40 * 2**20
    )
    return fused(n_dp, n_tp, *args) if fits else plain(*args)


def solution(mesh):
    return jax.shard_map(
        functools.partial(per_device, mesh.shape["dp"], mesh.shape["tp"]),
        mesh=mesh,
        in_specs=(
            P("dp", "tp", None),
            P(),
            P("dp", None, "tp"),
            P("dp", None, "tp"),
            P(None, "tp"),
            P(None, "tp"),
        ),
        out_specs=(P("dp", "tp", None), P()),
        check_vma=False,
    )
```

time: 29.3 us -> 25 us (0.85)
  Pallas kernels: 28.4 us -> 24.2 us
    pallas_call x1, Pallas kernels: 27.7 us -> 23.5 us  [fused(): pl.pallas_call(functools.partial(kernel, n_dp, n_tp), out_shape=(vmem(inp...]
where the time goes in v1:
time: 25 us; the launch traced here: 24.8 us
  Pallas kernels  24.2 us (97%)
  between operations  0.64 us (3%)
    pallas_call x1, Pallas kernels, fused(): pl.pallas_call(functools.partial(kernel, n_dp, n_tp), out_shape=(vmem(inp...  23.5 us
    pallas_call x1, Pallas kernels, fused(): pl.pallas_call(write_out, out_shape=(jax.ShapeDtypeStruct(inputs.shape, j...  0.64 us

profile of v1, /device:TPU:0, one launch (start us, length us, event | category | flops | bytes accessed | tf_op | source)
XLA Modules:
  0.0 24.8 jit_solution(14239388088225060350)
XLA Ops:
  0.6 23.5 %shard_map.77 = (bf16[1,1,8192]{2,1,0:T(2,128)(2,1)S(1)}, f32[32,1,256]{2,1,0:T(1,128)S(1)}) custom-call(bf16[1,1,8192]{2,1,0:T(2,128)(2,1)} %x_ref.1, f32[32,1,256]{2,1,0:T(1,128)} %bitcast.2, bf16[1,8,2048]{2,1,0:T(8,128)(2,1)} %gg_ref.1, bf16[1,8,2048]{2,1,0:T(8,128)(2,1)} %ug_ref.1, bf16[8192,2048]{1,0:T(8,128)(2,1)} %gw_ref.1, bf16[8192,2048]{1,0:T(8,128)(2,1)} %uw_ref.1), custom_call_target="tpu_custom_call" | custom-call | tf_op jit(solution)/shard_map/pallas_call | solution.py:268
  24.2 0.6 %shard_map.78 = (bf16[1,1,8192]{2,1,0:T(2,128)(2,1)}, f32[32,1,256]{2,1,0:T(1,128)}) custom-call(bf16[1,1,8192]{2,1,0:T(2,128)(2,1)S(1)} %get-tuple-element.6.dx_ref, f32[32,1,256]{2,1,0:T(1,128)S(1)} %get-tuple-element.7.dg_ref), custom_call_target="tpu_custom_call" | custom-call | tf_op jit(solution)/shard_map/pallas_call | solution.py:296

commit v2 on v1

--- a/solution.py
+++ b/solution.py
@@ -35,8 +35,8 @@
 
 def kernel(
     n_dp, n_tp, x_ref, gain_hbm, gg_ref, ug_ref, gw_ref, uw_ref, dx_ref, dg_ref,
-    w_buf, cot, g_mat, x_row, gain_ref, x_send, x_recv, x_mat, acc, part_send, part_recv, last_send, last_recv,
-    w_sem, own_sem, row_sem, known, cot_ss, cot_rs, x_ss, x_rs, part_ss, part_rs, last_ss, last_rs,
+    w_buf, cot, g_mat, x_row, gain_ref, x_send, x_recv, x_mat, acc, mine, scale_send, scale_recv, part_send, part_recv, last_send, last_recv,
+    w_sem, own_sem, known, cot_ss, cot_rs, x_ss, x_rs, part_ss, part_rs, last_ss, last_rs,
 ):
     n = n_dp * n_tp
     bits = n_tp.bit_length() - 1
@@ -57,14 +57,14 @@
     rows_of = [lax.rem(d + step, n_dp) for step in range(n_dp)]
 
     own = [
-        pltpu.make_async_copy(gg_ref.at[0], cot.at[d, 0], own_sem.at[0]),
-        pltpu.make_async_copy(ug_ref.at[0], cot.at[d, 1], own_sem.at[1]),
-        pltpu.make_async_copy(x_ref, x_row, row_sem.at[0]),
-        pltpu.make_async_copy(gain_hbm, gain_ref, row_sem.at[1]),
+        pltpu.make_async_copy(gg_ref.at[0], cot.at[0, d], own_sem.at[0]),
+        pltpu.make_async_copy(ug_ref.at[0], cot.at[1, d], own_sem.at[1]),
+        pltpu.make_async_copy(x_ref, x_row, own_sem.at[2]),
+        pltpu.make_async_copy(gain_hbm, gain_ref, own_sem.at[3]),
     ]
     with jax.named_scope("own_start"):
         for copy in own:
-            copy.start()
+            copy.start(priority=1)
 
     with jax.named_scope("greet"):
         barrier = pltpu.get_barrier_semaphore()
@@ -77,10 +77,20 @@
     order = sorted(range(n_tp), key=lambda k: -(k.bit_length()))
     half = n_tp // 2
 
+    def first_far(i, which):
+        return i < half and which == 0
+
     def weight_copy(i, which):
         rows = pl.ds(pl.multiple_of(base + partners[order[i]] * cut, cut), cut)
         source = (gw_ref, uw_ref)[which]
-        return pltpu.make_async_copy(source.at[rows, :], w_buf.at[i, which], w_sem.at[i, which])
+        slot = pl.ds((which * n_tp + i) * cut, cut)
+        return pltpu.make_async_copy(source.at[rows, :], w_buf.at[slot, :], w_sem.at[0 if first_far(i, which) else 1])
+
+    def weights_here(which):
+        low, count = ((0, half), (half, 2 * n_tp - half))[which]
+        return pltpu.make_async_copy(
+            gw_ref.at[pl.ds(0, count * cut), :], w_buf.at[pl.ds(low * cut, count * cut), :], w_sem.at[which]
+        )
 
     stream = [(i, 0) for i in range(half)] + [(i, 1) for i in range(half)]
     stream += [(i, which) for i in range(half, n_tp) for which in range(2)]
@@ -91,17 +101,14 @@
     def cot_copy(step, which):
         to = rows_of[step]
         return pltpu.make_async_remote_copy(
-            src_ref=cot.at[d, which], dst_ref=cot.at[d, which],
-            send_sem=cot_ss.at[which, to], recv_sem=cot_rs.at[which, d],
+            src_ref=cot.at[which, d], dst_ref=cot.at[which, d], send_sem=cot_ss, recv_sem=cot_rs.at[which],
             device_id={"dp": to, "tp": t}, device_id_type=MESH,
         )
 
-    def cot_arrival(step, which):
-        source = rows_of[step]
+    def cots(which):
         return pltpu.make_async_remote_copy(
-            src_ref=cot.at[source, which], dst_ref=cot.at[source, which],
-            send_sem=cot_ss.at[which, source], recv_sem=cot_rs.at[which, source],
-            device_id={"dp": source, "tp": t}, device_id_type=MESH,
+            src_ref=cot.at[which, pl.ds(0, n_dp - 1)], dst_ref=cot.at[which, pl.ds(0, n_dp - 1)], send_sem=cot_ss,
+            recv_sem=cot_rs.at[which], device_id={"dp": rows_of[1], "tp": t}, device_id_type=MESH,
         )
 
     with jax.named_scope("own_wait"):
@@ -117,11 +124,27 @@
     def tell(bit):
         pl.semaphore_signal(known.at[bit], inc=1, device_id={"dp": d, "tp": partners[2**bit]}, device_id_type=MESH)
 
-    def part_copy(i):
-        return pltpu.make_async_remote_copy(
-            src_ref=part_send.at[i], dst_ref=part_recv.at[i], send_sem=part_ss.at[i], recv_sem=part_rs.at[i],
-            device_id={"dp": d, "tp": partners[order[i]]}, device_id_type=MESH,
-        )
+    groups = [(0, half), (half, n_tp - 2), (n_tp - 2, n_tp - 1)]
+
+    def part_copies(i):
+        group = [low <= i < high for low, high in groups].index(True)
+        return [
+            pltpu.make_async_remote_copy(
+                src_ref=send.at[i], dst_ref=recv.at[i], send_sem=part_ss.at[which], recv_sem=part_rs.at[which, group],
+                device_id={"dp": d, "tp": partners[order[i]]}, device_id_type=MESH,
+            )
+            for which, (send, recv) in enumerate(((scale_send, scale_recv), (part_send, part_recv)))
+        ]
+
+    def parts(low, high, group):
+        return [
+            pltpu.make_async_remote_copy(
+                src_ref=send.at[pl.ds(low, high - low)], dst_ref=recv.at[pl.ds(low, high - low)],
+                send_sem=part_ss.at[which], recv_sem=part_rs.at[which, group],
+                device_id={"dp": d, "tp": partners[1]}, device_id_type=MESH,
+            )
+            for which, (send, recv) in enumerate(((scale_send, scale_recv), (part_send, part_recv)))
+        ]
 
     place = t * n_dp + d
 
@@ -144,15 +167,29 @@
         )
 
     def gather(which):
-        for step in range(1, n_dp):
-            cot_arrival(step, which).wait_recv()
+        cots(which).wait_recv()
         for row in range(n_dp):
-            g_mat[which, row * seq:(row + 1) * seq, :] = cot[row, which]
+            g_mat[which, row * seq:(row + 1) * seq, :] = cot[which, row]
+
+    def encode(i, cols, part):
+        most = jnp.maximum(jnp.max(jnp.abs(part), axis=0, keepdims=True), 1e-30)
+        scale_send[i, :, cols] = most * 2.0**-15
+        root = part * (2.0**15 / most)
+        square = root * root
+        fourth = square * square
+        part_send[i, :, cols] = (fourth * square * root * jnp.abs(root)).astype(jnp.bfloat16)
+
+    def decode(i):
+        power = part_recv[i].astype(jnp.float32)
+        back = lax.rsqrt(lax.rsqrt(lax.rsqrt(jnp.maximum(jnp.abs(power), 2.0**-126))))
+        square = back * back
+        return power * (square * square * square * back) * scale_recv[i]
 
     lanes = [slice(low, low + cut // 2) for low in range(0, cut, cut // 2)]
 
     def product(i, which, rows):
-        return lax.dot_general(w_buf[i, which, rows, :], g_mat[which], NT, preferred_element_type=jnp.float32)
+        low = (which * n_tp + i) * cut + rows.start
+        return lax.dot_general(w_buf[low:low + cut // 2, :], g_mat[which], NT, preferred_element_type=jnp.float32)
 
     tell(1)
     with jax.named_scope("x_norm"):
@@ -175,37 +212,35 @@
             pl.semaphore_signal(known.at[0], inc=1, device_id={"dp": rows_of[step], "tp": t}, device_id_type=MESH)
     with jax.named_scope("gather0"):
         gather(0)
-        for i in range(half):
-            weight_copy(i, 0).wait()
+        weights_here(0).wait()
     with jax.named_scope("gate_far"):
         for i in range(half):
             for rows in lanes:
                 acc[i, rows, :] = product(i, 0, rows)
-    with jax.named_scope("known"):
+    with jax.named_scope("x_start"):
         pl.semaphore_wait(known.at[0], n_dp - 1)
-    with jax.named_scope("x_start"):
         for k in range(n - 1):
             spread(x_send, x_recv, x_ss, x_rs, k).start()
     with jax.named_scope("gather1"):
         gather(1)
-        for i in range(half):
-            weight_copy(i, 1).wait()
-    with jax.named_scope("up_far"):
+        weights_here(1).wait()
+    with jax.named_scope("products"):
         for i in range(half):
             for rows in lanes:
-                part_send[i, :, rows] = (acc[i, rows, :] + product(i, 1, rows)).T
-            part_copy(i).start()
-    with jax.named_scope("w_wait"):
-        for i in range(half, n_tp):
-            for which in range(2):
-                weight_copy(i, which).wait()
-    with jax.named_scope("near"):
+                encode(i, rows, (acc[i, rows, :] + product(i, 1, rows)).T)
+            for copy in part_copies(i):
+                copy.start()
         for i in range(half, n_tp):
             for rows in lanes:
-                part_send[i, :, rows] = (product(i, 0, rows) + product(i, 1, rows)).T
+                part = (product(i, 0, rows) + product(i, 1, rows)).T
+                if i < n_tp - 1:
+                    encode(i, rows, part)
+                else:
+                    mine[:, rows] = part
             if i < n_tp - 1:
-                part_copy(i).start()
-    total = part_send[n_tp - 1]
+                for copy in part_copies(i):
+                    copy.start()
+    total = mine[...]
 
     with jax.named_scope("x_wait"):
         all_of(x_send, x_recv, x_ss, x_rs).wait_recv()
@@ -213,10 +248,12 @@
         for i in range(n):
             x_mat[i:i + 1, :] = x_recv[i]
 
-    for i in reversed(range(n_tp - 1)):
-        with jax.named_scope(f"part{i}"):
-            part_copy(i).wait_recv()
-            total = total + part_recv[i]
+    for group, (low, high) in enumerate(groups):
+        with jax.named_scope(f"part{group}"):
+            for copy in parts(low, high, group):
+                copy.wait_recv()
+            for i in range(low, high):
+                total = total + decode(i)
 
     with jax.named_scope("gain_part"):
         gain_part = jnp.sum(total * x_mat[...], axis=0, keepdims=True)
@@ -232,10 +269,9 @@
     with jax.named_scope("send_waits"):
         own[3].wait()
         for which in range(2):
-            for step in range(1, n_dp):
-                cot_copy(step, which).wait_send()
-        for i in range(n_tp - 1):
-            part_copy(i).wait_send()
+            cots(which).wait_send()
+        for copy in parts(0, n_tp - 1, 0):
+            copy.wait_send()
         all_of(x_send, x_recv, x_ss, x_rs).wait_send()
         all_of(last_send, last_recv, last_ss, last_rs).wait_send()
 
@@ -271,8 +307,8 @@
         in_specs=[pl.BlockSpec(memory_space=pl.ANY)] * 6,
         out_specs=(pl.BlockSpec(memory_space=vmem),) * 2,
         scratch_shapes=[
-            vmem((n_tp, 2, cut, depth), jnp.bfloat16),
-            vmem((n_dp, 2, seq, depth), jnp.bfloat16),
+            vmem((2 * n_tp * cut, depth), jnp.bfloat16),
+            vmem((2, n_dp, seq, depth), jnp.bfloat16),
             vmem((2, rows, depth), jnp.bfloat16),
             vmem(inputs.shape, jnp.bfloat16),
             vmem((n, 1, cut), jnp.float32),
@@ -280,15 +316,18 @@
             vmem((n, 1, cut), jnp.float32),
             vmem((n, cut), jnp.float32),
             vmem((n_tp // 2, cut, rows), jnp.float32),
-            vmem((n_tp, rows, cut), jnp.float32),
-            vmem((n_tp, rows, cut), jnp.float32),
+            vmem((rows, cut), jnp.float32),
+            vmem((n_tp, 1, cut), jnp.float32),
+            vmem((n_tp, 1, cut), jnp.float32),
+            vmem((n_tp, rows, cut), jnp.bfloat16),
+            vmem((n_tp, rows, cut), jnp.bfloat16),
             vmem((n, 2, 1, cut), jnp.float32),
             vmem((n, 2, 1, cut), jnp.float32),
-            dma((n_tp, 2)), dma((2,)), dma((2,)),
-            pltpu.SemaphoreType.REGULAR((n_tp.bit_length(),)),
-            dma((2, n_dp)), dma((2, n_dp)),
+            dma((2,)), dma((4,)),
+            pltpu.SemaphoreType.REGULAR((n_tp.bit_length() - 1,)),
+            dma, dma((2,)),
             dma, dma,
-            dma((n_tp,)), dma((n_tp,)),
+            dma((2,)), dma((2, 3)),
             dma, dma,
         ],
         compiler_params=pltpu.CompilerParams(collective_id=0, has_side_effects=True),

time: 25 us -> 22.7 us (0.908)
  Pallas kernels: 24.2 us -> 21.9 us
    pallas_call x1, Pallas kernels: 23.5 us -> 21.3 us  [fused(): pl.pallas_call(functools.partial(kernel, n_dp, n_tp), out_shape=(vmem(inp...]
where the time goes in v2:
time: 22.7 us; the launch traced here: 22.6 us
  Pallas kernels  21.9 us (96%)
  between operations  0.64 us (3%)
    pallas_call x1, Pallas kernels, fused(): pl.pallas_call(functools.partial(kernel, n_dp, n_tp), out_shape=(vmem(inp...  21.3 us
    pallas_call x1, Pallas kernels, fused(): pl.pallas_call(write_out, out_shape=(jax.ShapeDtypeStruct(inputs.shape, j...  0.64 us

profile of v2, /device:TPU:0, one launch (start us, length us, event | category | flops | bytes accessed | tf_op | source)
XLA Modules:
  0.0 22.6 jit_solution(7159725060805554359)
XLA Ops:
  0.6 21.3 %shard_map.77 = (bf16[1,1,8192]{2,1,0:T(2,128)(2,1)S(1)}, f32[32,1,256]{2,1,0:T(1,128)S(1)}) custom-call(bf16[1,1,8192]{2,1,0:T(2,128)(2,1)} %x_ref.1, f32[32,1,256]{2,1,0:T(1,128)} %bitcast.2, bf16[1,8,2048]{2,1,0:T(8,128)(2,1)} %gg_ref.1, bf16[1,8,2048]{2,1,0:T(8,128)(2,1)} %ug_ref.1, bf16[8192,2048]{1,0:T(8,128)(2,1)} %gw_ref.1, bf16[8192,2048]{1,0:T(8,128)(2,1)} %uw_ref.1), custom_call_target="tpu_custom_call" | custom-call | tf_op jit(solution)/shard_map/pallas_call | solution.py:304
  21.9 0.6 %shard_map.78 = (bf16[1,1,8192]{2,1,0:T(2,128)(2,1)}, f32[32,1,256]{2,1,0:T(1,128)}) custom-call(bf16[1,1,8192]{2,1,0:T(2,128)(2,1)S(1)} %get-tuple-element.6.dx_ref, f32[32,1,256]{2,1,0:T(1,128)S(1)} %get-tuple-element.7.dg_ref), custom_call_target="tpu_custom_call" | custom-call | tf_op jit(solution)/shard_map/pallas_call | solution.py:335

commit v3 on v2

--- a/solution.py
+++ b/solution.py
@@ -66,13 +66,27 @@
         for copy in own:
             copy.start(priority=1)
 
+    spot, line = lax.div(t, 2), n_tp // 2
+    beside = lax.min(spot, 1) + lax.min(line - 1 - spot, 1)
+
+    def signal(sem, to_d, to_t):
+        pl.semaphore_signal(sem, inc=1, device_id={"dp": to_d, "tp": to_t}, device_id_type=MESH)
+
+    def signal_line(sem):
+        @pl.when(spot > 0)
+        def _():
+            signal(sem, d, t - 2)
+
+        @pl.when(spot < line - 1)
+        def _():
+            signal(sem, d, t + 2)
+
     with jax.named_scope("greet"):
         barrier = pltpu.get_barrier_semaphore()
-        for bit in range(bits):
-            pl.semaphore_signal(barrier, inc=1, device_id={"dp": d, "tp": partners[2**bit]}, device_id_type=MESH)
         for step in range(1, n_dp):
-            pl.semaphore_signal(barrier, inc=1, device_id={"dp": rows_of[step], "tp": t}, device_id_type=MESH)
-
+            signal(barrier, rows_of[step], t)
+        signal(barrier, d, partners[1])
+        signal_line(barrier)
 
     order = sorted(range(n_tp), key=lambda k: -(k.bit_length()))
     half = n_tp // 2
@@ -115,14 +129,11 @@
         own[0].wait()
         own[1].wait()
     with jax.named_scope("bar_wait"):
-        pl.semaphore_wait(barrier, bits + n_dp - 1)
+        pl.semaphore_wait(barrier, n_dp + beside)
     with jax.named_scope("cot_start"):
         for which in range(2):
             for step in range(1, n_dp):
                 cot_copy(step, which).start()
-
-    def tell(bit):
-        pl.semaphore_signal(known.at[bit], inc=1, device_id={"dp": d, "tp": partners[2**bit]}, device_id_type=MESH)
 
     groups = [(0, half), (half, n_tp - 2), (n_tp - 2, n_tp - 1)]
 
@@ -191,7 +202,8 @@
         low = (which * n_tp + i) * cut + rows.start
         return lax.dot_general(w_buf[low:low + cut // 2, :], g_mat[which], NT, preferred_element_type=jnp.float32)
 
-    tell(1)
+    signal_line(known.at[1])
+    signal(known.at[1], d, partners[1])
     with jax.named_scope("x_norm"):
         own[2].wait()
         squares = jnp.zeros((1, cut), jnp.float32)
@@ -204,12 +216,14 @@
             x_send[i] = x_send[i] * inv_rms
         x_recv[me] = x_send[me]
     with jax.named_scope("rounds"):
-        for bit in range(1, bits):
-            pl.semaphore_wait(known.at[bit], 1)
-            if bit + 1 < bits:
-                tell(bit + 1)
-        for step in range(1, n_dp):
-            pl.semaphore_signal(known.at[0], inc=1, device_id={"dp": rows_of[step], "tp": t}, device_id_type=MESH)
+        for step in range(1, line - 1):
+            pl.semaphore_wait(known.at[step], beside + (1 if step == 1 else 0))
+            if step + 1 < line - 1:
+                signal_line(known.at[step + 1])
+        for step in range(n_dp):
+            for side in range(2):
+                if step or side:
+                    signal(known.at[0], rows_of[step], partners[side])
     with jax.named_scope("gather0"):
         gather(0)
         weights_here(0).wait()
@@ -218,26 +232,25 @@
             for rows in lanes:
                 acc[i, rows, :] = product(i, 0, rows)
     with jax.named_scope("x_start"):
-        pl.semaphore_wait(known.at[0], n_dp - 1)
+        pl.semaphore_wait(known.at[0], 2 * n_dp - 1)
         for k in range(n - 1):
             spread(x_send, x_recv, x_ss, x_rs, k).start()
     with jax.named_scope("gather1"):
         gather(1)
         weights_here(1).wait()
     with jax.named_scope("products"):
-        for i in range(half):
-            for rows in lanes:
-                encode(i, rows, (acc[i, rows, :] + product(i, 1, rows)).T)
-            for copy in part_copies(i):
-                copy.start()
-        for i in range(half, n_tp):
-            for rows in lanes:
-                part = (product(i, 0, rows) + product(i, 1, rows)).T
-                if i < n_tp - 1:
-                    encode(i, rows, part)
-                else:
-                    mine[:, rows] = part
-            if i < n_tp - 1:
+        for low, high in ((0, half), (half, n_tp - 1), (n_tp - 1, n_tp)):
+            for i in range(low, high):
+                for rows in lanes:
+                    if i < half:
+                        part = (acc[i, rows, :] + product(i, 1, rows)).T
+                    else:
+                        part = (product(i, 0, rows) + product(i, 1, rows)).T
+                    if i < n_tp - 1:
+                        encode(i, rows, part)
+                    else:
+                        mine[:, rows] = part
+            for i in range(low, min(high, n_tp - 1)):
                 for copy in part_copies(i):
                     copy.start()
     total = mine[...]
@@ -289,9 +302,15 @@
             dx_ref[0, :, i * cut:(i + 1) * cut] = (inv_rms * (scaled - x_send[i] * inner)).astype(jnp.bfloat16)
 
 
-def write_out(dx_ref, dg_ref, dx_out, dg_out):
-    dx_out[...] = dx_ref[...]
-    dg_out[...] = dg_ref[...]
+def write_out(dx_ref, dg_ref, dx_out, dg_out, sem):
+    copies = [
+        pltpu.make_async_copy(dg_ref, dg_out, sem.at[0]),
+        pltpu.make_async_copy(dx_ref, dx_out, sem.at[1]),
+    ]
+    for copy in copies:
+        copy.start()
+    for copy in copies:
+        copy.wait()
 
 
 def fused(n_dp, n_tp, inputs, norm_gain, gate_grad, up_grad, gate_weight, up_weight):
@@ -324,7 +343,7 @@
             vmem((n, 2, 1, cut), jnp.float32),
             vmem((n, 2, 1, cut), jnp.float32),
             dma((2,)), dma((4,)),
-            pltpu.SemaphoreType.REGULAR((n_tp.bit_length() - 1,)),
+            pltpu.SemaphoreType.REGULAR((n_tp // 2 - 1,)),
             dma, dma((2,)),
             dma, dma,
             dma((2,)), dma((2, 3)),
@@ -339,7 +358,8 @@
             jax.ShapeDtypeStruct((n, 1, cut), jnp.float32),
         ),
         in_specs=[pl.BlockSpec(memory_space=vmem)] * 2,
-        out_specs=(pl.BlockSpec(memory_space=vmem),) * 2,
+        out_specs=(pl.BlockSpec(memory_space=pl.ANY),) * 2,
+        scratch_shapes=[dma((2,))],
         compiler_params=pltpu.CompilerParams(vmem_limit_bytes=2**20),
     )(input_grad, gain_grad)
     return (input_grad, gain_grad.reshape(width))

time: 22.7 us -> 22.4 us (0.987)
  Pallas kernels: 21.9 us -> 21.6 us
    pallas_call x1, Pallas kernels: 21.3 us -> 21 us  [fused(): pl.pallas_call(functools.partial(kernel, n_dp, n_tp), out_shape=(vmem(inp...]
where the time goes in v3:
time: 22.4 us; the launch traced here: 22.3 us
  Pallas kernels  21.6 us (96%)
  between operations  0.64 us (3%)
    pallas_call x1, Pallas kernels, fused(): pl.pallas_call(functools.partial(kernel, n_dp, n_tp), out_shape=(vmem(inp...  21 us
    pallas_call x1, Pallas kernels, fused(): pl.pallas_call(write_out, out_shape=(jax.ShapeDtypeStruct(inputs.shape, j...  0.64 us

profile of v3, /device:TPU:0, one launch (start us, length us, event | category | flops | bytes accessed | tf_op | source)
XLA Modules:
  0.0 22.3 jit_solution(13684806929763441634)
XLA Ops:
  0.6 21.0 %shard_map.77 = (bf16[1,1,8192]{2,1,0:T(2,128)(2,1)S(1)}, f32[32,1,256]{2,1,0:T(1,128)S(1)}) custom-call(bf16[1,1,8192]{2,1,0:T(2,128)(2,1)} %x_ref.1, f32[32,1,256]{2,1,0:T(1,128)} %bitcast.2, bf16[1,8,2048]{2,1,0:T(8,128)(2,1)} %gg_ref.1, bf16[1,8,2048]{2,1,0:T(8,128)(2,1)} %ug_ref.1, bf16[8192,2048]{1,0:T(8,128)(2,1)} %gw_ref.1, bf16[8192,2048]{1,0:T(8,128)(2,1)} %uw_ref.1), custom_call_target="tpu_custom_call" | custom-call | tf_op jit(solution)/shard_map/pallas_call | solution.py:323
  21.6 0.6 %shard_map.78 = (bf16[1,1,8192]{2,1,0:T(2,128)(2,1)}, f32[32,1,256]{2,1,0:T(1,128)}) custom-call(bf16[1,1,8192]{2,1,0:T(2,128)(2,1)S(1)} %get-tuple-element.6.dx_ref, f32[32,1,256]{2,1,0:T(1,128)S(1)} %get-tuple-element.7.dg_ref), custom_call_target="tpu_custom_call" | custom-call | tf_op jit(solution)/shard_map/pallas_call | solution.py:354

commit v4 on v3

--- a/solution.py
+++ b/solution.py
@@ -135,7 +135,7 @@
             for step in range(1, n_dp):
                 cot_copy(step, which).start()
 
-    groups = [(0, half), (half, n_tp - 2), (n_tp - 2, n_tp - 1)]
+    groups = [(0, half), (half, n_tp - 1)]
 
     def part_copies(i):
         group = [low <= i < high for low, high in groups].index(True)
@@ -164,8 +164,8 @@
         to_t = lax.div(flat, n_dp)
         return flat - to_t * n_dp, to_t
 
-    def spread(send, recv, send_sem, recv_sem, k):
-        to_d, to_t = other(k)
+    def spread(send, recv, send_sem, recv_sem, to):
+        to_d, to_t = to
         return pltpu.make_async_remote_copy(
             src_ref=send.at[to_d * n_tp + to_t], dst_ref=recv.at[me], send_sem=send_sem, recv_sem=recv_sem,
             device_id={"dp": to_d, "tp": to_t}, device_id_type=MESH,
@@ -233,13 +233,15 @@
                 acc[i, rows, :] = product(i, 0, rows)
     with jax.named_scope("x_start"):
         pl.semaphore_wait(known.at[0], 2 * n_dp - 1)
-        for k in range(n - 1):
-            spread(x_send, x_recv, x_ss, x_rs, k).start()
+        for side in range(n_tp):
+            for step in range(n_dp):
+                if side or step:
+                    spread(x_send, x_recv, x_ss, x_rs, (rows_of[step], partners[n_tp - side if side else 0])).start()
     with jax.named_scope("gather1"):
         gather(1)
         weights_here(1).wait()
     with jax.named_scope("products"):
-        for low, high in ((0, half), (half, n_tp - 1), (n_tp - 1, n_tp)):
+        for low, high in ((0, half // 2), (half // 2, half), (half, n_tp - 1), (n_tp - 1, n_tp)):
             for i in range(low, high):
                 for rows in lanes:
                     if i < half:
@@ -275,7 +277,7 @@
             last_send[i, 1] = gain_part
     with jax.named_scope("last_start"):
         for k in range(n - 1):
-            spread(last_send, last_recv, last_ss, last_rs, k).start()
+            spread(last_send, last_recv, last_ss, last_rs, other(k)).start()
 
         last_recv[me] = last_send[me]
 
@@ -346,7 +348,7 @@
             pltpu.SemaphoreType.REGULAR((n_tp // 2 - 1,)),
             dma, dma((2,)),
             dma, dma,
-            dma((2,)), dma((2, 3)),
+            dma((2,)), dma((2, 2)),
             dma, dma,
         ],
         compiler_params=pltpu.CompilerParams(collective_id=0, has_side_effects=True),

time: 22.4 us -> 22.3 us (level)
  no operation moved by 1% of the time
where the time goes in v4:
time: 22.3 us; the launch traced here: 22.2 us
  Pallas kernels  21.5 us (96%)
  between operations  0.64 us (3%)
    pallas_call x1, Pallas kernels, fused(): pl.pallas_call(functools.partial(kernel, n_dp, n_tp), out_shape=(vmem(inp...  20.9 us
    pallas_call x1, Pallas kernels, fused(): pl.pallas_call(write_out, out_shape=(jax.ShapeDtypeStruct(inputs.shape, j...  0.64 us

profile of v4, /device:TPU:0, one launch (start us, length us, event | category | flops | bytes accessed | tf_op | source)
XLA Modules:
  0.0 22.2 jit_solution(17037886619252672782)
XLA Ops:
  0.6 20.9 %shard_map.77 = (bf16[1,1,8192]{2,1,0:T(2,128)(2,1)S(1)}, f32[32,1,256]{2,1,0:T(1,128)S(1)}) custom-call(bf16[1,1,8192]{2,1,0:T(2,128)(2,1)} %x_ref.1, f32[32,1,256]{2,1,0:T(1,128)} %bitcast.2, bf16[1,8,2048]{2,1,0:T(8,128)(2,1)} %gg_ref.1, bf16[1,8,2048]{2,1,0:T(8,128)(2,1)} %ug_ref.1, bf16[8192,2048]{1,0:T(8,128)(2,1)} %gw_ref.1, bf16[8192,2048]{1,0:T(8,128)(2,1)} %uw_ref.1), custom_call_target="tpu_custom_call" | custom-call | tf_op jit(solution)/shard_map/pallas_call | solution.py:325
  21.5 0.6 %shard_map.78 = (bf16[1,1,8192]{2,1,0:T(2,128)(2,1)}, f32[32,1,256]{2,1,0:T(1,128)}) custom-call(bf16[1,1,8192]{2,1,0:T(2,128)(2,1)S(1)} %get-tuple-element.6.dx_ref, f32[32,1,256]{2,1,0:T(1,128)S(1)} %get-tuple-element.7.dg_ref), custom_call_target="tpu_custom_call" | custom-call | tf_op jit(solution)/shard_map/pallas_call | solution.py:356
